TPU v7x, 32 devices: a whole 2x2x4 slice. The times are simulated.
32 devices in a mesh: owner: 4 (over z), rows: 8 (over y, x, core).
Axes of the slice: x: 2, y: 2, z: 4, core: 2. Of those that a mesh axis runs over, the one named last changes fastest.
Arguments:
- w_gate: float32 [128, 2048, 768], P('owner', 'rows'), may hold values from -0.1875 to 0.1875
- w_up: float32 [128, 2048, 768], P('owner', 'rows'), may hold values from -0.1875 to 0.1875
- router_weight: float32 [2048, 128], P('rows', 'owner'), may hold values from -0.125 to 0.125
- router_gain: float32 [2048], P('rows'), may hold values from 0.25 to 1.75
Outputs:
- serve_gate: bfloat16 [128, 2048, 768], P('owner', None, 'rows')
- serve_up: bfloat16 [128, 2048, 768], P('owner', None, 'rows')
- scale_gate: float32 [128, 768], P('owner', 'rows')
- scale_up: float32 [128, 768], P('owner', 'rows')
- serve_router: bfloat16 [2048, 128], replicated
All inputs are finite; a program needn't handle non-finite values. Where the computation divides by a largest or mean magnitude, that divisor is 1e-20 or more.
Results may differ from a plain program's by a relative error of at most 0.001.
Values may be sent and summed in bfloat16 or wider, within the bound.
No kernel may reach another device: no remote copies, remote signals or barrier semaphores. Data moves between devices by JAX's collectives and lax.ppermute only.
A program may use at most 192 MiB of HBM per device.

v0:
```python
import jax
import jax.numpy as jnp
from jax import lax
from jax.sharding import PartitionSpec as P

D_MODEL = 2048


def on_device(w_gate, w_up, router_weight, router_gain):
    total_gate, total_up = lax.psum(
        (jnp.sum(jnp.abs(w_gate), axis=1), jnp.sum(jnp.abs(w_up), axis=1)), "rows"
    )
    scale_gate = total_gate / D_MODEL
    scale_up = total_up / D_MODEL
    narrow_gate, narrow_up = (
        (w_gate / jnp.expand_dims(scale_gate, 1)).astype(jnp.bfloat16),
        (w_up / jnp.expand_dims(scale_up, 1)).astype(jnp.bfloat16),
    )
    serve_gate, serve_up = (
        lax.all_to_all(narrow_gate, "rows", split_axis=2, concat_axis=1, tiled=True),
        lax.all_to_all(narrow_up, "rows", split_axis=2, concat_axis=1, tiled=True),
    )
    scale_gate = lax.dynamic_slice_in_dim(
        scale_gate, lax.axis_index("rows") * serve_gate.shape[2], serve_gate.shape[2], axis=1
    )
    scale_up = lax.dynamic_slice_in_dim(
        scale_up, lax.axis_index("rows") * serve_up.shape[2], serve_up.shape[2], axis=1
    )
    part_router = (router_weight * router_gain[:, None]).astype(jnp.bfloat16)
    row_router = lax.all_gather(part_router, "rows", axis=0, tiled=True)
    serve_router = lax.all_gather(row_router, "owner", axis=1, tiled=True)
    return (serve_gate, serve_up, scale_gate, scale_up, serve_router)


def solution(mesh):
    placed = (P("owner", "rows", None), P("owner", "rows", None), P("rows", "owner"), P("rows"))
    return jax.shard_map(
        on_device,
        mesh=mesh,
        in_specs=placed,
        out_specs=(
            P("owner", None, "rows"),
            P("owner", None, "rows"),
            P("owner", "rows"),
            P("owner", "rows"),
            P(),
        ),
        check_vma=False,
    )
```

profile of v0, /device:TPU:0, one launch (start us, length us, event | category | flops | bytes accessed | tf_op | source)
XLA Modules:
  0.0 481.1 jit_solution(11326135817132377053)
XLA Ops:
  7.2 0.0 all-reduce.3.cloned.1.call-start
  7.2 17.4 %abs_reduce_fusion = (f32[32,768]{1,0:T(8,128)}, f32[32,768]{1,0:T(8,128)}) fusion(f32[32,256,768]{2,1,0:T(8,128)} %param.5, f32[32,256,768]{2,1,0:T(8,128)} %param.4), kind=kLoop, calls=%fused_computation.1 | loop fusion | flops 25116672 | bytes 50528256 | tf_op jit(solution)/shard_map/reduce_sum | solution.py:11
  24.6 0.0 all-reduce.3.cloned.1.call-update
  24.7 25.1 %copy.25 = f32[32,256,768]{1,0,2:T(8,128)} copy(f32[32,256,768]{2,1,0:T(8,128)} %param.5) | data formatting | bytes 50331648 | tf_op args[1]
  49.8 31.5 %all-reduce.3.cloned.1.call-done = (f32[32,768]{1,0:T(8,128)}, f32[32,768]{1,0:T(8,128)}) async-done(((f32[32,768]{1,0:T(8,128)}, f32[32,768]{1,0:T(8,128)}), (f32[32,768]{1,0:T(8,128)}, f32[32,768]{1,0:T(8,128)})) %all-reduce.3.cloned.1.call-update) | async-done | bytes 196624 | tf_op jit(solution)/shard_map/psum | solution.py:10
  81.3 0.9 broadcast_multiply_fusion
  82.2 0.2 copy.24
  82.4 14.1 %divide_convert_fusion = bf16[32,256,768]{1,0,2:T(8,128)(2,1)} fusion(f32[32,256,768]{1,0,2:T(8,128)} %copy.25, f32[32,768]{0,1:T(8,128)S(1)} %copy.24), kind=kLoop, calls=%fused_computation | loop fusion | flops 12582912 | bytes 37847040 | tf_op jit(solution)/shard_map/convert_element_type | solution.py:17
  96.5 5.4 %all-to-all-start.1 = ((bf16[32,256,768]{1,0,2:T(8,128)(2,1)}), bf16[32,256,768]{1,0,2:T(8,128)(2,1)}, u32[]{:S(2)}, u32[]{:S(2)}) async-start(bf16[32,256,768]{1,0,2:T(8,128)(2,1)} %divide_convert_fusion), calls=%async_computation.1 | async-start | bytes 25165824 | tf_op jit(solution)/shard_map/all_to_all | solution.py:21
  101.9 0.0 copy-start
  101.9 25.1 %copy.21 = f32[32,256,768]{1,0,2:T(8,128)} copy(f32[32,256,768]{2,1,0:T(8,128)} %param.4) | data formatting | bytes 50331648 | tf_op args[0]
  127.1 0.0 copy-done
  127.1 0.2 copy.20
  127.2 0.0 copy-start.1
  127.3 0.0 copy-start.2
  127.3 14.1 %divide_convert_fusion.1 = bf16[32,256,768]{1,0,2:T(8,128)(2,1)} fusion(f32[32,256,768]{1,0,2:T(8,128)} %copy.21, f32[32,768]{0,1:T(8,128)S(1)} %copy.20), kind=kLoop, calls=%fused_computation.2 | loop fusion | flops 12582912 | bytes 37847040 | tf_op jit(solution)/shard_map/convert_element_type | solution.py:16
  141.4 99.5 %all-to-all-done.1 = bf16[32,256,768]{1,0,2:T(8,128)(2,1)} async-done(((bf16[32,256,768]{1,0,2:T(8,128)(2,1)}), bf16[32,256,768]{1,0,2:T(8,128)(2,1)}, u32[]{:S(2)}, u32[]{:S(2)}) %all-to-all-start.1) | async-done | bytes 12582944 | tf_op jit(solution)/shard_map/all_to_all | solution.py:21
  240.9 5.4 %all-to-all-start = ((bf16[32,256,768]{1,0,2:T(8,128)(2,1)}), bf16[32,256,768]{1,0,2:T(8,128)(2,1)}, u32[]{:S(2)}, u32[]{:S(2)}) async-start(bf16[32,256,768]{1,0,2:T(8,128)(2,1)} %divide_convert_fusion.1), calls=%async_computation | async-start | bytes 25165824 | tf_op jit(solution)/shard_map/all_to_all | solution.py:20
  246.3 0.0 copy-done.1
  246.3 0.0 copy-done.2
  246.3 142.4 %all_gather.6 = bf16[2048,32]{0,1:T(8,128)(2,1)S(1)} all-gather(bf16[256,32]{0,1:T(8,128)(2,1)S(1)} %multiply_convert_fusion), channel_id=1, replica_groups=mesh['owner'=4,'rows'=8] {'rows'}, dimensions={0}, use_global_device_ids=true | all-gather | bytes 147456 | tf_op jit(solution)/shard_map/all_gather | solution.py:30
  388.8 16.1 %all_gather.7 = bf16[2048,128]{0,1:T(8,128)(2,1)S(1)} all-gather(bf16[2048,32]{0,1:T(8,128)(2,1)S(1)} %all_gather.6), channel_id=1, replica_groups=mesh['owner'=4,'rows'=8] {'owner'}, dimensions={1}, use_global_device_ids=true | all-gather | bytes 655360 | tf_op jit(solution)/shard_map/all_gather | solution.py:31
  404.8 1.0 copy.28
  405.8 0.7 constant_dynamic-slice_fusion
  406.5 0.7 constant_dynamic-slice_fusion.1
  407.2 14.1 %copy.27 = bf16[32,8,256,96]{2,1,3,0:T(8,128)(2,1)} copy(bf16[32,8,256,96]{2,0,3,1:T(8,128)(2,1)} %bitcast.5) | data formatting | bytes 25165824 | tf_op jit(solution)/shard_map/all_to_all | solution.py:21
  421.2 19.5 %all_to_all.33 = bf16[32,2048,96]{1,2,0:T(8,128)(2,1)} reshape(bf16[32,8,256,96]{2,1,3,0:T(8,128)(2,1)} %copy.27) | data formatting | bytes 25165824 | tf_op jit(solution)/shard_map/all_to_all | solution.py:21
  440.7 0.0 all-to-all-done
  440.7 14.1 %copy.23 = bf16[32,8,256,96]{2,1,3,0:T(8,128)(2,1)} copy(bf16[32,8,256,96]{2,0,3,1:T(8,128)(2,1)} %bitcast.2) | data formatting | bytes 25165824 | tf_op jit(solution)/shard_map/all_to_all | solution.py:20
  454.8 19.5 %all_to_all.29 = bf16[32,2048,96]{1,2,0:T(8,128)(2,1)} reshape(bf16[32,8,256,96]{2,1,3,0:T(8,128)(2,1)} %copy.23) | data formatting | bytes 25165824 | tf_op jit(solution)/shard_map/all_to_all | solution.py:20
  (2 shorter events, 0.0 us)
Async XLA Ops:
  7.2 74.2 %all-reduce.3.cloned.1.call-start = ((), (), s32[]{:S(2)}) async-start(), calls=%async_computation.2 | async-start | bytes 393216 | tf_op jit(solution)/shard_map/psum | solution.py:10
  96.5 144.4 %all-to-all-start.1 = ((bf16[32,256,768]{1,0,2:T(8,128)(2,1)}), bf16[32,256,768]{1,0,2:T(8,128)(2,1)}, u32[]{:S(2)}, u32[]{:S(2)}) async-start(bf16[32,256,768]{1,0,2:T(8,128)(2,1)} %divide_convert_fusion), calls=%async_computation.1 | async-start | bytes 25165824 | tf_op jit(solution)/shard_map/all_to_all | solution.py:21
  101.9 25.1 %copy-start = (f32[32,768]{1,0:T(8,128)S(1)}, f32[32,768]{1,0:T(8,128)}, u32[]{:S(2)}) copy-start(f32[32,768]{1,0:T(8,128)} %get-tuple-element.10) | copy-start | bytes 294916
  127.2 119.0 %copy-start.1 = (f32[256,32]{0,1:T(8,128)S(1)}, f32[256,32]{0,1:T(8,128)}, u32[]{:S(2)}) copy-start(f32[256,32]{0,1:T(8,128)} %param.6) | copy-start | bytes 98308
  127.3 119.0 %copy-start.2 = (f32[256]{0:T(256)S(1)}, f32[256]{0:T(256)}, u32[]{:S(2)}) copy-start(f32[256]{0:T(256)} %param.7) | copy-start | bytes 3076
  240.9 199.8 %all-to-all-start = ((bf16[32,256,768]{1,0,2:T(8,128)(2,1)}), bf16[32,256,768]{1,0,2:T(8,128)(2,1)}, u32[]{:S(2)}, u32[]{:S(2)}) async-start(bf16[32,256,768]{1,0,2:T(8,128)(2,1)} %divide_convert_fusion.1), calls=%async_computation | async-start | bytes 25165824 | tf_op jit(solution)/shard_map/all_to_all | solution.py:20
Sparse Core Ops, SparseCore 0:
  24.8 56.4 all-reduce.2
where the time goes:
time: 483 us; the launch traced here: 481 us
  blocking collectives  158 us (33%)
  waiting for transfers between devices  131 us (27%)
  local copies, waits for them, and re-layouts  120 us (25%)
  other arithmetic  46.6 us (10%)
  between operations  14.1 us (3%)
  starting transfers between devices  10.8 us (2%)
    all_gather x1, blocking collectives, on_device(): row_router = lax.all_gather(part_router, 'rows', axis=0, tiled=True)  142 us
    all_to_all x1, waiting for transfers between devices, on_device(): lax.all_to_all(narrow_up, 'rows', split_axis=2, concat_axis=1, tiled=True)  99.5 us
    unnamed x9, local copies, waits for them, and re-layouts  51.3 us
    all_to_all x2, local copies, waits for them, and re-layouts, on_device(): lax.all_to_all(narrow_gate, 'rows', split_axis=2, concat_axis=1, tiled=True)  33.6 us
    all_to_all x2, local copies, waits for them, and re-layouts, on_device(): lax.all_to_all(narrow_up, 'rows', split_axis=2, concat_axis=1, tiled=True)  33.6 us
    psum x1, waiting for transfers between devices, on_device(): lax.psum((jnp.sum(jnp.abs(w_gate), axis=1), jnp.sum(jnp.abs(w_up), axis=1...  31.5 us
    reduce_sum x1, other arithmetic, on_device(): jnp.sum(jnp.abs(w_up), axis=1)  17.4 us
    all_gather x1, blocking collectives, on_device(): serve_router = lax.all_gather(row_router, 'owner', axis=1, tiled=True)  16.1 us
  transfers between devices with their start and end apart: 3, of which 2 were waited for; matrix products, arithmetic and copies ran while one was open for 17% of the time, Pallas kernels for 0%

commit v1 on v0

--- a/solution.py
+++ b/solution.py
@@ -1,9 +1,20 @@
+import functools
 import jax
 import jax.numpy as jnp
 from jax import lax
 from jax.sharding import PartitionSpec as P
+from jax.lax import all_gather
 
 D_MODEL = 2048
+
+
+def _supply_all_block(array_in, dev_axis, ndim_at):
+    back = all_gather(array_in, dev_axis)
+    moved = jnp.concatenate(back, axis=ndim_at)
+    return moved
+
+
+rails_wait = functools.partial(_supply_all_block, dev_axis="owner", ndim_at=1)
 
 
 def on_device(w_gate, w_up, router_weight, router_gain):
@@ -28,7 +39,7 @@
     )
     part_router = (router_weight * router_gain[:, None]).astype(jnp.bfloat16)
     row_router = lax.all_gather(part_router, "rows", axis=0, tiled=True)
-    serve_router = lax.all_gather(row_router, "owner", axis=1, tiled=True)
+    serve_router = rails_wait(row_router)
     return (serve_gate, serve_up, scale_gate, scale_up, serve_router)
 
 

time: 483 us -> 484 us (level)
  no operation moved by 1% of the time
where the time goes in v1:
time: 484 us; the launch traced here: 482 us
  blocking collectives  158 us (33%)
  waiting for transfers between devices  131 us (27%)
  local copies, waits for them, and re-layouts  121 us (25%)
  other arithmetic  46.6 us (10%)
  between operations  14.1 us (3%)
  starting transfers between devices  10.8 us (2%)
    all_gather x1, blocking collectives, on_device(): row_router = lax.all_gather(part_router, 'rows', axis=0, tiled=True)  142 us
    all_to_all x1, waiting for transfers between devices, on_device(): lax.all_to_all(narrow_up, 'rows', split_axis=2, concat_axis=1, tiled=True)  99.5 us
    unnamed x9, local copies, waits for them, and re-layouts  51.3 us
    all_to_all x2, local copies, waits for them, and re-layouts, on_device(): lax.all_to_all(narrow_gate, 'rows', split_axis=2, concat_axis=1, tiled=True)  33.6 us
    all_to_all x2, local copies, waits for them, and re-layouts, on_device(): lax.all_to_all(narrow_up, 'rows', split_axis=2, concat_axis=1, tiled=True)  33.6 us
    psum x1, waiting for transfers between devices, on_device(): lax.psum((jnp.sum(jnp.abs(w_gate), axis=1), jnp.sum(jnp.abs(w_up), axis=1...  31.5 us
    reduce_sum x1, other arithmetic, on_device(): jnp.sum(jnp.abs(w_up), axis=1)  17.4 us
    all_gather x1, blocking collectives, _supply_all_block(): back = all_gather(array_in, dev_axis)  16.1 us
  transfers between devices with their start and end apart: 3, of which 2 were waited for; matrix products, arithmetic and copies ran while one was open for 17% of the time, Pallas kernels for 0%

profile of v1, /device:TPU:0, one launch (start us, length us, event | category | flops | bytes accessed | tf_op | source)
XLA Modules:
  0.0 481.8 jit_solution(18065938339496638089)
XLA Ops:
  7.2 0.0 all-reduce.3.cloned.1.call-start
  7.2 17.4 %abs_reduce_fusion = (f32[32,768]{1,0:T(8,128)}, f32[32,768]{1,0:T(8,128)}) fusion(f32[32,256,768]{2,1,0:T(8,128)} %param.5, f32[32,256,768]{2,1,0:T(8,128)} %param.4), kind=kLoop, calls=%fused_computation.1 | loop fusion | flops 25116672 | bytes 50528256 | tf_op jit(solution)/shard_map/reduce_sum | solution.py:22
  24.6 0.0 all-reduce.3.cloned.1.call-update
  24.7 25.1 %copy.26 = f32[32,256,768]{1,0,2:T(8,128)} copy(f32[32,256,768]{2,1,0:T(8,128)} %param.5) | data formatting | bytes 50331648 | tf_op args[1]
  49.8 31.5 %all-reduce.3.cloned.1.call-done = (f32[32,768]{1,0:T(8,128)}, f32[32,768]{1,0:T(8,128)}) async-done(((f32[32,768]{1,0:T(8,128)}, f32[32,768]{1,0:T(8,128)}), (f32[32,768]{1,0:T(8,128)}, f32[32,768]{1,0:T(8,128)})) %all-reduce.3.cloned.1.call-update) | async-done | bytes 196624 | tf_op jit(solution)/shard_map/psum | solution.py:21
  81.3 0.9 broadcast_multiply_fusion
  82.2 0.2 copy.25
  82.4 14.1 %divide_convert_fusion = bf16[32,256,768]{1,0,2:T(8,128)(2,1)} fusion(f32[32,256,768]{1,0,2:T(8,128)} %copy.26, f32[32,768]{0,1:T(8,128)S(1)} %copy.25), kind=kLoop, calls=%fused_computation | loop fusion | flops 12582912 | bytes 37847040 | tf_op jit(solution)/shard_map/convert_element_type | solution.py:28
  96.5 5.4 %all-to-all-start.1 = ((bf16[32,256,768]{1,0,2:T(8,128)(2,1)}), bf16[32,256,768]{1,0,2:T(8,128)(2,1)}, u32[]{:S(2)}, u32[]{:S(2)}) async-start(bf16[32,256,768]{1,0,2:T(8,128)(2,1)} %divide_convert_fusion), calls=%async_computation.1 | async-start | bytes 25165824 | tf_op jit(solution)/shard_map/all_to_all | solution.py:32
  101.9 0.0 copy-start
  101.9 25.1 %copy.22 = f32[32,256,768]{1,0,2:T(8,128)} copy(f32[32,256,768]{2,1,0:T(8,128)} %param.4) | data formatting | bytes 50331648 | tf_op args[0]
  127.1 0.0 copy-done
  127.1 0.2 copy.21
  127.2 0.0 copy-start.1
  127.3 0.0 copy-start.2
  127.3 14.1 %divide_convert_fusion.1 = bf16[32,256,768]{1,0,2:T(8,128)(2,1)} fusion(f32[32,256,768]{1,0,2:T(8,128)} %copy.22, f32[32,768]{0,1:T(8,128)S(1)} %copy.21), kind=kLoop, calls=%fused_computation.2 | loop fusion | flops 12582912 | bytes 37847040 | tf_op jit(solution)/shard_map/convert_element_type | solution.py:27
  141.4 99.5 %all-to-all-done.1 = bf16[32,256,768]{1,0,2:T(8,128)(2,1)} async-done(((bf16[32,256,768]{1,0,2:T(8,128)(2,1)}), bf16[32,256,768]{1,0,2:T(8,128)(2,1)}, u32[]{:S(2)}, u32[]{:S(2)}) %all-to-all-start.1) | async-done | bytes 12582944 | tf_op jit(solution)/shard_map/all_to_all | solution.py:32
  240.9 5.4 %all-to-all-start = ((bf16[32,256,768]{1,0,2:T(8,128)(2,1)}), bf16[32,256,768]{1,0,2:T(8,128)(2,1)}, u32[]{:S(2)}, u32[]{:S(2)}) async-start(bf16[32,256,768]{1,0,2:T(8,128)(2,1)} %divide_convert_fusion.1), calls=%async_computation | async-start | bytes 25165824 | tf_op jit(solution)/shard_map/all_to_all | solution.py:31
  246.3 0.0 copy-done.1
  246.3 0.0 copy-done.2
  246.3 142.4 %all_gather.9 = bf16[2048,32]{0,1:T(8,128)(2,1)S(1)} all-gather(bf16[256,32]{0,1:T(8,128)(2,1)S(1)} %multiply_convert_fusion), channel_id=1, replica_groups=mesh['owner'=4,'rows'=8] {'rows'}, dimensions={0}, use_global_device_ids=true | all-gather | bytes 147456 | tf_op jit(solution)/shard_map/all_gather | solution.py:41
  388.8 16.1 %all-gather = bf16[8192,32]{0,1:T(8,128)(2,1)S(1)} all-gather(bf16[2048,32]{0,1:T(8,128)(2,1)S(1)} %all_gather.9), channel_id=2, replica_groups=mesh['owner'=4,'rows'=8] {'owner'}, dimensions={0}, use_global_device_ids=true | all-gather | bytes 655360 | tf_op jit(solution)/shard_map/all_gather | solution.py:12
  404.8 0.4 reshape.21
  405.2 0.3 copy.29
  405.5 1.0 copy.30
  406.5 0.7 constant_dynamic-slice_fusion
  407.2 0.7 constant_dynamic-slice_fusion.1
  407.8 14.1 %copy.28 = bf16[32,8,256,96]{2,1,3,0:T(8,128)(2,1)} copy(bf16[32,8,256,96]{2,0,3,1:T(8,128)(2,1)} %bitcast.5) | data formatting | bytes 25165824 | tf_op jit(solution)/shard_map/all_to_all | solution.py:32
  421.9 19.5 %all_to_all.33 = bf16[32,2048,96]{1,2,0:T(8,128)(2,1)} reshape(bf16[32,8,256,96]{2,1,3,0:T(8,128)(2,1)} %copy.28) | data formatting | bytes 25165824 | tf_op jit(solution)/shard_map/all_to_all | solution.py:32
  441.4 0.0 all-to-all-done
  441.4 14.1 %copy.24 = bf16[32,8,256,96]{2,1,3,0:T(8,128)(2,1)} copy(bf16[32,8,256,96]{2,0,3,1:T(8,128)(2,1)} %bitcast.2) | data formatting | bytes 25165824 | tf_op jit(solution)/shard_map/all_to_all | solution.py:31
  455.5 19.5 %all_to_all.29 = bf16[32,2048,96]{1,2,0:T(8,128)(2,1)} reshape(bf16[32,8,256,96]{2,1,3,0:T(8,128)(2,1)} %copy.24) | data formatting | bytes 25165824 | tf_op jit(solution)/shard_map/all_to_all | solution.py:31
  (2 shorter events, 0.0 us)
Async XLA Ops:
  7.2 74.2 %all-reduce.3.cloned.1.call-start = ((), (), s32[]{:S(2)}) async-start(), calls=%async_computation.2 | async-start | bytes 393216 | tf_op jit(solution)/shard_map/psum | solution.py:21
  96.5 144.4 %all-to-all-start.1 = ((bf16[32,256,768]{1,0,2:T(8,128)(2,1)}), bf16[32,256,768]{1,0,2:T(8,128)(2,1)}, u32[]{:S(2)}, u32[]{:S(2)}) async-start(bf16[32,256,768]{1,0,2:T(8,128)(2,1)} %divide_convert_fusion), calls=%async_computation.1 | async-start | bytes 25165824 | tf_op jit(solution)/shard_map/all_to_all | solution.py:32
  101.9 25.1 %copy-start = (f32[32,768]{1,0:T(8,128)S(1)}, f32[32,768]{1,0:T(8,128)}, u32[]{:S(2)}) copy-start(f32[32,768]{1,0:T(8,128)} %get-tuple-element.20) | copy-start | bytes 294916
  127.2 119.0 %copy-start.1 = (f32[256,32]{0,1:T(8,128)S(1)}, f32[256,32]{0,1:T(8,128)}, u32[]{:S(2)}) copy-start(f32[256,32]{0,1:T(8,128)} %param.6) | copy-start | bytes 98308
  127.3 119.0 %copy-start.2 = (f32[256]{0:T(256)S(1)}, f32[256]{0:T(256)}, u32[]{:S(2)}) copy-start(f32[256]{0:T(256)} %param.7) | copy-start | bytes 3076
  240.9 200.5 %all-to-all-start = ((bf16[32,256,768]{1,0,2:T(8,128)(2,1)}), bf16[32,256,768]{1,0,2:T(8,128)(2,1)}, u32[]{:S(2)}, u32[]{:S(2)}) async-start(bf16[32,256,768]{1,0,2:T(8,128)(2,1)} %divide_convert_fusion.1), calls=%async_computation | async-start | bytes 25165824 | tf_op jit(solution)/shard_map/all_to_all | solution.py:31
Sparse Core Ops, SparseCore 0:
  24.8 56.4 all-reduce.2
